TPU v7x, 32 devices: a whole 2x2x4 slice. The times are simulated.
32 devices in a mesh: dp: 8 (over z, core), fsdp: 4 (over y, x).
Axes of the slice: x: 2, y: 2, z: 4, core: 2. Of those that a mesh axis runs over, the one named last changes fastest.
Arguments:
- layer_input_tokens: bfloat16 [32768, 768], P(('dp', 'fsdp')), may hold values from -6 to 6
- cotangent: bfloat16 [32768, 768], P(('dp', 'fsdp')), may hold values from -6 to 6
- lengths: int32 [160], P(('dp', 'fsdp')), may hold values from 33 to 512, as said below
- query_key_value_weight: float32 [768, 2304], P(('dp', 'fsdp')), may hold values from -0.21875 to 0.21875
- output_weight: float32 [768, 768], P(('dp', 'fsdp')), may hold values from -0.875 to 0.875
- up_weight: float32 [768, 3072], P(('dp', 'fsdp')), may hold values from -0.21875 to 0.21875
- down_weight: float32 [3072, 768], P(('dp', 'fsdp')), may hold values from -0.109375 to 0.109375
- a_in: float32 [768, 40], P(('dp', 'fsdp')), may hold values from -0.21875 to 0.21875
- a_down: float32 [3072, 8], P(('dp', 'fsdp')), may hold values from -0.109375 to 0.109375
- ln_gains: float32 [2, 768], P(None, ('dp', 'fsdp')), may hold values from 0.5 to 1.5
- ln_biases: float32 [2, 768], P(None, ('dp', 'fsdp')), may hold values from -3 to 3
- adapter_b: float32 [8, 6912], replicated, may hold values from -0.3 to 0.3
- moment_one: float32 [8, 6912], replicated, may hold values from -0.72 to 0.72
- moment_two: float32 [8, 6912], replicated, may hold values from 0.005 to 0.05
Outputs:
- layer_out: bfloat16 [32768, 768], P(('dp', 'fsdp'))
- input_grad: bfloat16 [32768, 768], P(('dp', 'fsdp'))
- b_grad: float32 [8, 6912], replicated
- grad_norm: float32 [], replicated
- moment_one_new: float32 [8, 6912], replicated
- moment_two_new: float32 [8, 6912], replicated
- adapter_b_new: float32 [8, 6912], replicated
Inputs may be any that keep to these rules, and one draw needn't show every extreme that they name: `lengths`: item 5 j + i lies in bucket i of its set; its length is more than half of its bucket and at most the bucket. Some item has exactly 512 valid tokens.
All inputs are finite; a program needn't handle non-finite values.
Results may differ from a plain program's by a relative error of at most 0.012.
The roundings to bfloat16 on the way count: a program that leaves them out, or rounds other values in their place, can miss the bound.
Values may be sent and summed in bfloat16 or wider, within the bound.
A program may use at most 192 MiB of HBM per device.

v0:
```python
import jax
import jax.numpy as jnp
from jax import lax
from jax.sharding import PartitionSpec as P

HEAD = 64
ITEM_LEN = 512
STEP = 10
adapter_scale = 2.0
ln_eps = 1e-05
clip_norm = 256.0
beta_one = 0.9
beta_two = 0.98
learn_rate = 0.02
decay_rate = 0.01


def bucket_plan(full):
    return (
        (0, full, 1, 0),
        (full, full // 2, 1, 1),
        (full * 3 // 2, full // 4, 1, 2),
        (full * 7 // 4, full // 8, 2, 3),
    )


def keep_mask(lengths_set, full):
    parts = []
    for offset, size, count, first in bucket_plan(full):
        positions = jnp.arange(size, dtype=jnp.int32)
        bounds = lengths_set[:, first : first + count]
        mask = (positions[None, None, :] < bounds[:, :, None]).astype(jnp.float32)
        parts.append(mask.reshape(lengths_set.shape[0], count * size))
    return jnp.concatenate(parts, axis=1)


def product_result(left, right):
    return jnp.dot(left, right, preferred_element_type=jnp.float32)


def transposed_product(left, right):
    return lax.dot_general(
        left, right, (((1,), (1,)), ((), ())), preferred_element_type=jnp.float32
    )


def product_tn(left, right):
    return lax.dot_general(
        left, right, (((0,), (0,)), ((), ())), preferred_element_type=jnp.float32
    )


def norm_forward(resid, gain, shift):
    center = resid - jnp.mean(resid, axis=1, keepdims=True)
    variance = jnp.mean(center * center, axis=1, keepdims=True)
    inv_std = lax.rsqrt(variance + ln_eps)
    normed = center * inv_std
    return (normed * gain + shift, normed, inv_std)


def norm_backward(grad_out, normed, inv_std, gain):
    scaled = grad_out * gain
    return inv_std * (
        scaled
        - jnp.mean(scaled, axis=1, keepdims=True)
        - normed * jnp.mean(scaled * normed, axis=1, keepdims=True)
    )


def gelu_exact(values):
    return 0.5 * values * (1.0 + jax.scipy.special.erf(values * 0.7071067811865476))


def gelu_slope(values):
    normal_cdf = 0.5 * (1.0 + jax.scipy.special.erf(values * 0.7071067811865476))
    density = jnp.exp(-0.5 * values * values) * 0.3989422804014327
    return normal_cdf + values * density


def masked_scores(query, key_rows, keep_block):
    scores = (
        jnp.einsum("gqhe,gkhe->ghqk", query, key_rows, preferred_element_type=jnp.float32) * 0.125
    )
    return jnp.where(keep_block[:, None, None, :] > 0.5, scores, -1e30)


def bucket_forward(query, key_rows, value_rows, keep_block):
    scores = masked_scores(query, key_rows, keep_block)
    highest = jnp.max(scores, axis=-1, keepdims=True)
    expo = jnp.exp(scores - highest)
    totals = jnp.sum(expo, axis=-1, keepdims=True)
    probs = (expo / totals).astype(jnp.bfloat16)
    context_rows = jnp.einsum(
        "ghqk,gkhe->gqhe", probs, value_rows, preferred_element_type=jnp.float32
    )
    return (context_rows.astype(jnp.bfloat16), highest + jnp.log(totals))


def bucket_backward(query, key_rows, value_rows, keep_block, log_total, grad_ctx):
    scores = masked_scores(query, key_rows, keep_block)
    probs = jnp.exp(scores - log_total)
    grad_probs = jnp.einsum(
        "gqhe,gkhe->ghqk", grad_ctx, value_rows, preferred_element_type=jnp.float32
    )
    delta = jnp.sum(probs * grad_probs, axis=-1, keepdims=True)
    grad_scores = (probs * (grad_probs - delta)).astype(jnp.bfloat16)
    grad_query = (
        jnp.einsum("ghqk,gkhe->gqhe", grad_scores, key_rows, preferred_element_type=jnp.float32)
        * 0.125
    )
    grad_key = (
        jnp.einsum("ghqk,gqhe->gkhe", grad_scores, query, preferred_element_type=jnp.float32)
        * 0.125
    )
    grad_value = jnp.einsum(
        "ghqk,gqhe->gkhe", probs.astype(jnp.bfloat16), grad_ctx, preferred_element_type=jnp.float32
    )
    return (
        grad_query.astype(jnp.bfloat16),
        grad_key.astype(jnp.bfloat16),
        grad_value.astype(jnp.bfloat16),
    )


def set_forward(operands):
    query, key_rows, value_rows, lens = operands
    heads, size_head = (query.shape[1], query.shape[2])
    keep_set = keep_mask(lens[None, :], ITEM_LEN)[0]
    contexts = []
    totals = []
    for offset, size, count, first in bucket_plan(ITEM_LEN):
        span = count * size
        shape = (count, size, heads, size_head)
        context_rows, log_total = bucket_forward(
            query[offset : offset + span].reshape(shape),
            key_rows[offset : offset + span].reshape(shape),
            value_rows[offset : offset + span].reshape(shape),
            keep_set[offset : offset + span].reshape(count, size),
        )
        contexts.append(context_rows.reshape(span, heads, size_head))
        totals.append(log_total)
    return (jnp.concatenate(contexts, axis=0), tuple(totals))


def set_backward(operands):
    query, key_rows, value_rows, lens, log_totals, grad_ctx = operands
    heads, size_head = (query.shape[1], query.shape[2])
    keep_set = keep_mask(lens[None, :], ITEM_LEN)[0]
    grads_q = []
    grads_k = []
    grads_v = []
    for index, (offset, size, count, first) in enumerate(bucket_plan(ITEM_LEN)):
        span = count * size
        shape = (count, size, heads, size_head)
        grad_q, grad_k, grad_v = bucket_backward(
            query[offset : offset + span].reshape(shape),
            key_rows[offset : offset + span].reshape(shape),
            value_rows[offset : offset + span].reshape(shape),
            keep_set[offset : offset + span].reshape(count, size),
            log_totals[index],
            grad_ctx[offset : offset + span].reshape(shape),
        )
        grads_q.append(grad_q.reshape(span, heads, size_head))
        grads_k.append(grad_k.reshape(span, heads, size_head))
        grads_v.append(grad_v.reshape(span, heads, size_head))
    return (
        jnp.concatenate(grads_q, axis=0),
        jnp.concatenate(grads_k, axis=0),
        jnp.concatenate(grads_v, axis=0),
    )


def adam_update(gradient, grad_norm, moment_old, second_old, weights):
    clipped = gradient * jnp.minimum(1.0, clip_norm / (grad_norm + 1e-06))
    moment_new = beta_one * moment_old + (1.0 - beta_one) * clipped
    second_new = beta_two * second_old + (1.0 - beta_two) * clipped * clipped
    first_hat = moment_new / (1.0 - beta_one**STEP)
    second_hat = second_new / (1.0 - beta_two**STEP)
    weights_new = weights - learn_rate * (
        first_hat / (jnp.sqrt(second_hat) + 1e-08) + decay_rate * weights
    )
    return (moment_new, second_new, weights_new)


def on_device(
    layer_input_tokens,
    cotangent,
    lengths,
    query_key_value_weight,
    output_weight,
    up_weight,
    down_weight,
    a_in,
    a_down,
    ln_gains,
    ln_biases,
    adapter_b,
    moment_one,
    moment_two,
):
    total_rows, width = layer_input_tokens.shape
    span_all = 2 * ITEM_LEN
    sets = total_rows // span_all
    lowrank = adapter_b.shape[0]
    hidden = up_weight.shape[1]
    head_count = width // HEAD
    brain_float_type = jnp.bfloat16
    gathered = (
        lax.all_gather(
            query_key_value_weight.astype(brain_float_type), ("dp", "fsdp"), axis=0, tiled=True
        ),
        lax.all_gather(output_weight.astype(brain_float_type), ("dp", "fsdp"), axis=0, tiled=True),
        lax.all_gather(up_weight.astype(brain_float_type), ("dp", "fsdp"), axis=0, tiled=True),
        lax.all_gather(down_weight.astype(brain_float_type), ("dp", "fsdp"), axis=0, tiled=True),
        lax.all_gather(a_in.astype(brain_float_type), ("dp", "fsdp"), axis=0, tiled=True),
        lax.all_gather(a_down.astype(brain_float_type), ("dp", "fsdp"), axis=0, tiled=True),
        lax.all_gather(ln_gains.astype(brain_float_type), ("dp", "fsdp"), axis=1, tiled=True),
        lax.all_gather(ln_biases.astype(brain_float_type), ("dp", "fsdp"), axis=1, tiled=True),
    )
    (
        projection_weight_gradient,
        output_weight_gradient,
        up_weight_gradient,
        down_weight_gradient,
        g_ain,
        g_adown,
        g_gain,
        g_bias,
    ) = gathered
    gain_full = g_gain.astype(jnp.float32)
    bias_full = g_bias.astype(jnp.float32)
    lengths_set = lengths.reshape(sets, 5)
    keep = keep_mask(lengths_set, ITEM_LEN)
    keep_rows = keep.reshape(-1, 1)
    b_low = adapter_b.astype(brain_float_type)
    query_adapter_matrix = b_low[:, :width]
    key_adapter_matrix = b_low[:, width : 2 * width]
    value_adapter_matrix = b_low[:, 2 * width : 3 * width]
    attention_adapter_bias = b_low[:, 3 * width : 4 * width]
    upper_adapter_matrix = b_low[:, 4 * width : 4 * width + hidden]
    lower_adapter_matrix = b_low[:, 4 * width + hidden :]
    projection_down_matrix = product_result(layer_input_tokens, g_ain[:, : 3 * lowrank]).astype(
        brain_float_type
    )
    adapter_projection_delta = jnp.concatenate(
        [
            product_result(projection_down_matrix[:, :lowrank], query_adapter_matrix),
            product_result(projection_down_matrix[:, lowrank : 2 * lowrank], key_adapter_matrix),
            product_result(projection_down_matrix[:, 2 * lowrank :], value_adapter_matrix),
        ],
        axis=1,
    )
    query_key_value = (
        product_result(layer_input_tokens, projection_weight_gradient)
        + adapter_scale * adapter_projection_delta
    ).astype(brain_float_type)
    qkv_heads = query_key_value.reshape(sets, span_all, 3, head_count, HEAD)
    query = qkv_heads[:, :, 0]
    key_rows = qkv_heads[:, :, 1]
    value_rows = qkv_heads[:, :, 2]
    context_rows, log_totals = lax.map(set_forward, (query, key_rows, value_rows, lengths_set))
    context_token_rows = context_rows.reshape(sets * span_all, width)
    attention_down_matrix = product_result(
        context_token_rows, g_ain[:, 3 * lowrank : 4 * lowrank]
    ).astype(brain_float_type)
    attention_output = product_result(
        context_token_rows, output_weight_gradient
    ) + adapter_scale * product_result(attention_down_matrix, attention_adapter_bias)
    hidden_one, normed_one, inv_one = norm_forward(
        layer_input_tokens.astype(jnp.float32) + attention_output, gain_full[0], bias_full[0]
    )
    hidden_lower_rows = hidden_one.astype(brain_float_type)
    upper_down_matrix = product_result(hidden_lower_rows, g_ain[:, 4 * lowrank :]).astype(
        brain_float_type
    )
    upper_rows = product_result(
        hidden_lower_rows, up_weight_gradient
    ) + adapter_scale * product_result(upper_down_matrix, upper_adapter_matrix)
    active_rows = gelu_exact(upper_rows).astype(brain_float_type)
    lower_down_matrix = product_result(active_rows, g_adown).astype(brain_float_type)
    feedforward_output = product_result(
        active_rows, down_weight_gradient
    ) + adapter_scale * product_result(lower_down_matrix, lower_adapter_matrix)
    output, normed_two, inv_two = norm_forward(
        hidden_one + feedforward_output, gain_full[1], bias_full[1]
    )
    layer_out = (output * keep_rows).astype(brain_float_type)
    again = (
        lax.all_gather(
            query_key_value_weight.astype(brain_float_type), ("dp", "fsdp"), axis=0, tiled=True
        ),
        lax.all_gather(output_weight.astype(brain_float_type), ("dp", "fsdp"), axis=0, tiled=True),
        lax.all_gather(up_weight.astype(brain_float_type), ("dp", "fsdp"), axis=0, tiled=True),
        lax.all_gather(down_weight.astype(brain_float_type), ("dp", "fsdp"), axis=0, tiled=True),
        lax.all_gather(a_in.astype(brain_float_type), ("dp", "fsdp"), axis=0, tiled=True),
        lax.all_gather(a_down.astype(brain_float_type), ("dp", "fsdp"), axis=0, tiled=True),
        lax.all_gather(ln_gains.astype(brain_float_type), ("dp", "fsdp"), axis=1, tiled=True),
        lax.all_gather(ln_biases.astype(brain_float_type), ("dp", "fsdp"), axis=1, tiled=True),
    )
    (
        projection_weight_gradient,
        output_weight_gradient,
        up_weight_gradient,
        down_weight_gradient,
        g_ain,
        g_adown,
        g_gain,
        g_bias,
    ) = again
    gain_full = g_gain.astype(jnp.float32)
    grad_out = cotangent.astype(jnp.float32) * keep_rows
    grad_two = norm_backward(grad_out, normed_two, inv_two, gain_full[1])
    feedforward_gradient = grad_two.astype(brain_float_type)
    lower_down_gradient = (
        adapter_scale * transposed_product(feedforward_gradient, lower_adapter_matrix)
    ).astype(brain_float_type)
    grad_active = transposed_product(
        feedforward_gradient, down_weight_gradient
    ) + transposed_product(lower_down_gradient, g_adown)
    upper_output_gradient = (grad_active * gelu_slope(upper_rows)).astype(brain_float_type)
    upper_down_gradient = (
        adapter_scale * transposed_product(upper_output_gradient, upper_adapter_matrix)
    ).astype(brain_float_type)
    grad_hidden = (
        grad_two
        + transposed_product(upper_output_gradient, up_weight_gradient)
        + transposed_product(upper_down_gradient, g_ain[:, 4 * lowrank :])
    )
    grad_one = norm_backward(grad_hidden, normed_one, inv_one, gain_full[0])
    attention_gradient = grad_one.astype(brain_float_type)
    attention_down_gradient = (
        adapter_scale * transposed_product(attention_gradient, attention_adapter_bias)
    ).astype(brain_float_type)
    grad_ctx = (
        transposed_product(attention_gradient, output_weight_gradient)
        + transposed_product(attention_down_gradient, g_ain[:, 3 * lowrank : 4 * lowrank])
    ).astype(brain_float_type)
    grad_q, grad_k, grad_v = lax.map(
        set_backward,
        (
            query,
            key_rows,
            value_rows,
            lengths_set,
            log_totals,
            grad_ctx.reshape(sets, span_all, head_count, HEAD),
        ),
    )
    grad_qkv = jnp.stack([grad_q, grad_k, grad_v], axis=2).reshape(sets * span_all, 3 * width)
    grad_uqkv = (
        adapter_scale
        * jnp.concatenate(
            [
                transposed_product(grad_qkv[:, :width], query_adapter_matrix),
                transposed_product(grad_qkv[:, width : 2 * width], key_adapter_matrix),
                transposed_product(grad_qkv[:, 2 * width :], value_adapter_matrix),
            ],
            axis=1,
        )
    ).astype(brain_float_type)
    input_grad = (
        grad_one
        + transposed_product(grad_qkv, projection_weight_gradient)
        + transposed_product(grad_uqkv, g_ain[:, : 3 * lowrank])
    ).astype(brain_float_type)
    local_gradient = adapter_scale * jnp.concatenate(
        [
            product_tn(projection_down_matrix[:, :lowrank], grad_qkv[:, :width]),
            product_tn(
                projection_down_matrix[:, lowrank : 2 * lowrank], grad_qkv[:, width : 2 * width]
            ),
            product_tn(projection_down_matrix[:, 2 * lowrank :], grad_qkv[:, 2 * width :]),
            product_tn(attention_down_matrix, attention_gradient),
            product_tn(upper_down_matrix, upper_output_gradient),
            product_tn(lower_down_matrix, feedforward_gradient),
        ],
        axis=1,
    )
    b_grad = lax.psum(local_gradient, ("dp", "fsdp"))
    grad_norm = jnp.sqrt(jnp.sum(b_grad * b_grad))
    moment_new, second_new, adapter_new = adam_update(
        b_grad, grad_norm, moment_one, moment_two, adapter_b
    )
    return (layer_out, input_grad, b_grad, grad_norm, moment_new, second_new, adapter_new)


def solution(mesh):
    placed = (
        P(("dp", "fsdp"), None),
        P(("dp", "fsdp"), None),
        P(("dp", "fsdp")),
        P(("dp", "fsdp"), None),
        P(("dp", "fsdp"), None),
        P(("dp", "fsdp"), None),
        P(("dp", "fsdp"), None),
        P(("dp", "fsdp"), None),
        P(("dp", "fsdp"), None),
        P(None, ("dp", "fsdp")),
        P(None, ("dp", "fsdp")),
        P(),
        P(),
        P(),
    )
    return jax.shard_map(
        on_device,
        mesh=mesh,
        in_specs=placed,
        out_specs=(P(("dp", "fsdp"), None), P(("dp", "fsdp"), None), P(), P(), P(), P(), P()),
        check_vma=False,
    )
```

profile of v0, /device:TPU:8, one launch (start us, length us, event | category | flops | bytes accessed | tf_op | source)
XLA Modules:
  0.0 654.7 jit_solution(7428954899423333268)
XLA Ops:
  7.2 1.7 convert_element_type.392
  10.6 1.6 convert_element_type.423
  12.3 1.6 convert_element_type.426
  22.8 57.2 %all_gather.32 = bf16[768,40]{1,0:T(8,128)(2,1)S(1)} all-gather(bf16[24,40]{1,0:T(8,128)(2,1)S(1)} %convert_element_type.393), channel_id=1, replica_groups=mesh['dp'=8,'fsdp'=4] {'dp','fsdp'}, dimensions={0}, use_global_device_ids=true | all-gather | bytes 63360 | tf_op jit(solution)/shard_map/all_gather | solution.py:215
  80.0 1.6 copy.149
  82.1 2.3 fusion.119
  84.4 2.4 fusion.122
  86.8 2.3 fusion.125
  89.9 64.0 %all-gather.1 = bf16[32,24,2]{1,2,0:T(2,128)(2,1)S(1)} all-gather(bf16[1,24,2]{1,2,0:T(2,128)(2,1)S(1)} %convert_bitcast_fusion.1), channel_id=1, replica_groups=mesh['dp'=8,'fsdp'=4] {'dp','fsdp'}, dimensions={0}, use_global_device_ids=true | all-gather | bytes 3168 | tf_op jit(solution)/shard_map/all_gather | solution.py:218
  154.0 66.0 %all-gather = bf16[32,24,2]{1,2,0:T(2,128)(2,1)S(1)} all-gather(bf16[1,24,2]{1,2,0:T(2,128)(2,1)S(1)} %convert_bitcast_fusion.2), channel_id=1, replica_groups=mesh['dp'=8,'fsdp'=4] {'dp','fsdp'}, dimensions={0}, use_global_device_ids=true | all-gather | bytes 3168 | tf_op jit(solution)/shard_map/all_gather | solution.py:217
  221.7 63.5 %all-gather.2 = bf16[32,96,8]{1,2,0:T(8,128)(2,1)S(1)} all-gather(bf16[1,96,8]{1,2,0:T(8,128)(2,1)S(1)} %convert_bitcast_fusion), channel_id=1, replica_groups=mesh['dp'=8,'fsdp'=4] {'dp','fsdp'}, dimensions={0}, use_global_device_ids=true | all-gather | bytes 50688 | tf_op jit(solution)/shard_map/all_gather | solution.py:216
  285.9 1.6 copy.167
  288.1 8.8 %fusion.9 = bf16[1024,2304]{1,0:T(8,128)(2,1)} fusion(f32[1024,768]{1,0:T(8,128)} %fusion.119, f32[1024,768]{1,0:T(8,128)} %fusion.122, f32[1024,768]{1,0:T(8,128)} %fusion.125, bf16[1024,768]{1,0:T(8,128)(2,1)S(1)} %copy-done.17, bf16[768,2304]{1,0:T(8,128)(2,1)} %all-gather.8.cloned.1.call-done), kind=kOutput, calls=%fused_computation.20 | convolution fusion | flops 3635675136 | bytes 19267584 | tf_op jit(solution)/shard_map/dot_general | solution.py:38
  297.0 6.6 %copy.153 = bf16[1024,2304]{0,1:T(8,128)(2,1)} copy(bf16[1024,2304]{1,0:T(8,128)(2,1)} %fusion.9) | data formatting | bytes 9437184 | tf_op jit(solution)/shard_map/convert_element_type | solution.py:256
  312.3 1.9 fusion.156
  314.2 5.1 fusion.157
  319.8 2.0 fusion.47
  321.8 2.0 copy-done.64
  323.7 1.8 fusion.6
  325.5 4.0 fusion.25
  330.0 2.8 fusion.99
  338.4 7.5 %fusion.162 = f32[1024,3072]{1,0:T(8,128)S(1)} fusion(bf16[1024,768]{0,1:T(8,128)(2,1)} %copy-done.8, bf16[768,3072]{1,0:T(8,128)(2,1)} %all-gather.12.cloned.1.call-done), kind=kOutput, calls=%fused_computation.253 | convolution fusion | flops 4831838208 | bytes 18874368 | tf_op jit(solution)/shard_map/dot_general | solution.py:38
  345.9 7.2 %multiply_convert_fusion.1 = (bf16[1024,3072]{1,0:T(8,128)(2,1)S(1)}, f32[1024,3072]{1,0:T(8,128)}) fusion(f32[1024,3072]{1,0:T(8,128)S(1)} %fusion.162, bf16[1024,8]{0,1:T(8,128)(2,1)S(1)} %convolution_convert_fusion.6, bf16[8,6912]{1,0:T(8,128)(2,1)S(1)} %convert_element_type.395), kind=kOutput, calls=%fused_computation.10 | convolution fusion | flops 72351744 | bytes 31522816 | tf_op jit(solution)/shard_map/dot_general | solution.py:38
  353.1 2.7 copy-done.6
  355.8 1.7 convolution_convert_fusion.5
  357.5 8.8 %fusion.163 = f32[1024,768]{0,1:T(8,128)S(1)} fusion(bf16[1024,3072]{1,0:T(8,128)(2,1)} %copy-done.6, bf16[3072,768]{1,0:T(8,128)(2,1)} %all-gather.14.cloned.1.call-done), kind=kOutput, calls=%fused_computation.254 | convolution fusion | flops 4831838208 | bytes 14155776 | tf_op jit(solution)/shard_map/dot_general | solution.py:38
  367.9 2.1 copy-done.5
  370.9 2.6 fusion.108
  373.5 8.0 %fusion.164 = f32[1024,3072]{1,0:T(8,128)} fusion(bf16[1024,768]{0,1:T(8,128)(2,1)S(1)} %get-tuple-element.118, bf16[3072,768]{1,0:T(8,128)(2,1)S(1)} %bitcast.280), kind=kOutput, calls=%fused_computation.255 | convolution fusion | flops 4831838208 | bytes 18874368 | tf_op jit(solution)/shard_map/dot_general | solution.py:42
  381.5 13.7 %fusion.5 = bf16[1024,3072]{1,0:T(8,128)(2,1)} fusion(f32[1024,3072]{1,0:T(8,128)} %get-tuple-element.136, f32[1024,3072]{1,0:T(8,128)} %fusion.164, bf16[3072,8]{0,1:T(8,128)(2,1)S(1)} %copy-done.47, bf16[1024,768]{0,1:T(8,128)(2,1)} %copy-done.18, bf16[8,6912]{1,0:T(8,128)(2,1)S(1)} %convert_element_type.395), kind=kOutput, calls=%fused_computation.6 | convolution fusion | flops 97533952 | bytes 33091584 | tf_op jit(solution)/shard_map/dot_general | solution.py:42
  395.2 10.0 %fusion.165 = f32[1024,768]{0,1:T(8,128)} fusion(bf16[1024,3072]{1,0:T(8,128)(2,1)} %fusion.5, bf16[768,3072]{1,0:T(8,128)(2,1)} %all-gather.12.cloned.1.call-done), kind=kOutput, calls=%fused_computation.256 | convolution fusion | flops 4831838208 | bytes 14155776 | tf_op jit(solution)/shard_map/dot_general | solution.py:42
  405.2 10.2 %fusion.149 = (f32[1024]{0:T(1024)S(1)}, f32[1024]{0:T(1024)S(1)}, f32[1024,768]{0,1:T(8,128)}) fusion(f32[1024]{0:T(1024)S(1)} %copy-done.53, f32[1024,768]{0,1:T(8,128)S(1)} %get-tuple-element.134, f32[1024]{0:T(1024)S(1)} %broadcast_multiply_fusion.6, f32[768]{0:T(1024)S(1)} %copy-done.62, bf16[768,40]{1,0:T(8,128)(2,1)S(1)} %all_gather.32, ...), kind=kOutput, calls=%fused_computation.243 | convolution fusion | flops 76298240 | bytes 20738048 | tf_op jit(solution)/shard_map/dot_general | solution.py:42
  415.5 2.8 fusion.84
  419.5 3.0 fusion.166
  422.5 4.4 add_convert_fusion.1
  426.9 1.8 slice.306
  428.7 1.7 fusion.152
  430.4 2.1 slice.305
  432.5 1.9 reshape.739
  434.4 1.7 fusion.54
  436.1 1.7 multiply_reduce_fusion.6
  442.8 2.0 fusion.64
  444.8 1.9 fusion.65
  448.1 1.9 multiply_reduce_fusion.1
  450.7 2.6 fusion.55
  453.3 2.2 fusion.56
  455.5 3.2 fusion.38
  458.7 7.1 %multiply_reduce_fusion = (f32[12,512]{1,0:T(8,128)S(1)}, f32[12,512,512]{1,2,0:T(8,128)}) fusion(f32[12,512,512]{1,2,0:T(8,128)S(1)} %bitcast.240, f32[12,512]{1,0:T(8,128)S(1)} %copy-done.39, bf16[512,12,64]{0,2,1:T(8,128)(2,1)S(1)} %bitcast.267, bf16[1,1024,3,12,64]{1,4,3,2,0:T(8,128)(2,1)} %bitcast.254), kind=kOutput, calls=%fused_computation.8 | convolution fusion | flops 412084224 | bytes 26787840 | tf_op jit(solution)/shard_map/while/body/eval_jaxpr/gqhe,gkhe->ghqk/dot_general | solution.py:102
  465.8 6.8 %multiply_convert_fusion = bf16[12,512,512]{1,2,0:T(8,128)(2,1)S(1)} fusion(f32[12,512,512]{1,2,0:T(8,128)} %get-tuple-element.147, f32[12,512,512]{1,2,0:T(8,128)S(1)} %bitcast.240, f32[12,512]{1,0:T(8,128)S(1)} %get-tuple-element.146, f32[12,512]{1,0:T(8,128)S(1)} %copy-done.39), kind=kLoop, calls=%fused_computation.7 | loop fusion | flops 12582912 | bytes 31506432 | tf_op jit(solution)/shard_map/while/body/eval_jaxpr/convert_element_type | solution.py:106
  472.6 4.0 fusion.43
  476.7 3.1 fusion.42
  481.0 1.9 reshape.748
  482.9 1.9 copy.176
  484.8 1.9 reshape.740
  486.7 1.9 copy.183
  488.6 1.9 reshape.744
  490.6 1.7 maximum_bitcast_fusion.2
  494.9 2.6 fusion.32
  503.4 6.9 %fusion.167 = f32[1024,768]{0,1:T(8,128)S(1)} fusion(bf16[768,2304]{1,0:T(8,128)(2,1)} %all-gather.8.cloned.1.call-done, bf16[1024,2304]{0,1:T(8,128)(2,1)} %bitcast.265), kind=kOutput, calls=%fused_computation.258 | convolution fusion | flops 3623878656 | bytes 11403264 | tf_op jit(solution)/shard_map/dot_general | solution.py:42
  510.4 2.3 add_convert_fusion
  512.7 2.7 copy.192
  517.0 123.7 %all-reduce.2.cloned.1.call-done = f32[8,6912]{1,0:T(8,128)} async-done(((f32[8,6912]{1,0:T(8,128)}), f32[8,6912]{1,0:T(8,128)}) %all-reduce.2.cloned.1.call-update) | async-done | bytes 221200 | tf_op jit(solution)/shard_map/psum | solution.py:379
  643.1 1.9 multiply_subtract_fusion
  644.9 1.6 copy.241
  (284 shorter events, 53.2 us)
Async XLA Ops:
  7.2 72.8 %copy-start.17 = (bf16[1024,768]{1,0:T(8,128)(2,1)S(1)}, bf16[1024,768]{1,0:T(8,128)(2,1)}, u32[]{:S(2)}) copy-start(bf16[1024,768]{1,0:T(8,128)(2,1)} %param.14) | copy-start | bytes 4718596
  7.2 281.0 %all-gather.8.cloned.1.call-start = ((), (), s32[]{:S(2)}) async-start(), calls=%async_computation | async-start | bytes 3649536 | tf_op jit(solution)/shard_map/all_gather | solution.py:209
  8.9 321.0 %all-gather.10.cloned.1.call-start = ((), (), s32[]{:S(2)}) async-start(), calls=%async_computation.1 | async-start | bytes 1216512 | tf_op jit(solution)/shard_map/all_gather | solution.py:212
  10.5 327.8 %all-gather.12.cloned.1.call-start = ((), (), s32[]{:S(2)}) async-start(), calls=%async_computation.2 | async-start | bytes 4866048 | tf_op jit(solution)/shard_map/all_gather | solution.py:213
  12.2 345.3 %all-gather.14.cloned.1.call-start = ((), (), s32[]{:S(2)}) async-start(), calls=%async_computation.3 | async-start | bytes 4866048 | tf_op jit(solution)/shard_map/all_gather | solution.py:214
  13.9 626.8 %all-reduce.2.cloned.1.call-start = ((), (), s32[]{:S(2)}) async-start(), calls=%async_computation.4 | async-start | bytes 442368 | tf_op jit(solution)/shard_map/psum | solution.py:379
  22.8 399.7 %copy-start.38 = (bf16[8,6912]{1,0:T(8,128)(2,1)}, bf16[8,6912]{1,0:T(8,128)(2,1)S(1)}, u32[]{:S(2)}) copy-start(bf16[8,6912]{1,0:T(8,128)(2,1)S(1)} %convert_element_type.395) | copy-start | bytes 331780
  82.1 4.7 copy-start.40
  84.4 5.4 copy-start.81
  84.4 5.4 copy-start.82
  84.4 5.5 copy-start.77
  84.4 201.5 %copy-start.26 = (bf16[1024,768]{1,0:T(8,128)(2,1)S(1)}, bf16[1024,768]{1,0:T(8,128)(2,1)}, u32[]{:S(2)}) copy-start(bf16[1024,768]{1,0:T(8,128)(2,1)} %param.15) | copy-start | bytes 4718596
  220.9 115.4 %copy-start.61 = (f32[768]{0:T(1024)}, f32[768]{0:T(1024)S(1)}, u32[]{:S(2)}) copy-start(f32[768]{0:T(1024)S(1)} %get-tuple-element.109) | copy-start | bytes 9220
  305.0 5.0 copy-start.28
  305.2 4.8 copy-start.30
  305.4 4.6 copy-start.83
  305.8 4.8 copy-start.27
  314.2 5.6 copy-start.2
  319.3 6.2 copy-start
  319.8 4.0 copy-start.64
  325.5 4.0 copy-start.56
  330.0 2.9 copy-start.58
  330.0 2.9 copy-start.20
  333.8 81.7 %copy-start.45 = (f32[1024]{0:T(1024)}, f32[1024]{0:T(1024)S(1)}, u32[]{:S(2)}) copy-start(f32[1024]{0:T(1024)S(1)} %broadcast_multiply_fusion.6) | copy-start | bytes 12292
  334.4 3.9 copy-start.52
  338.3 7.5 %copy-start.48 = (bf16[1024,8]{0,1:T(8,128)(2,1)}, bf16[1024,8]{0,1:T(8,128)(2,1)S(1)}, u32[]{:S(2)}) copy-start(bf16[1024,8]{0,1:T(8,128)(2,1)S(1)} %convolution_convert_fusion.6) | copy-start | bytes 49156
  345.9 9.9 %copy-start.47 = (bf16[3072,8]{0,1:T(8,128)(2,1)S(1)}, bf16[3072,8]{0,1:T(8,128)(2,1)}, u32[]{:S(2)}) copy-start(bf16[3072,8]{0,1:T(8,128)(2,1)} %reshape.756) | copy-start | bytes 147460
  357.5 8.9 %copy-start.50 = (bf16[1024,8]{0,1:T(8,128)(2,1)}, bf16[1024,8]{0,1:T(8,128)(2,1)S(1)}, u32[]{:S(2)}) copy-start(bf16[1024,8]{0,1:T(8,128)(2,1)S(1)} %convolution_convert_fusion.5) | copy-start | bytes 49156
  357.5 8.9 %copy-start.53 = (f32[1024]{0:T(1024)S(1)}, f32[1024]{0:T(1024)}, u32[]{:S(2)}) copy-start(f32[1024]{0:T(1024)} %copy-done.52) | copy-start | bytes 12292
  357.5 8.9 %copy-start.62 = (f32[768]{0:T(1024)S(1)}, f32[768]{0:T(1024)}, u32[]{:S(2)}) copy-start(f32[768]{0:T(1024)} %copy-done.61) | copy-start | bytes 9220
  357.5 8.9 %copy-start.69 = (f32[768]{0:T(1024)S(1)}, f32[768]{0:T(1024)}, u32[]{:S(2)}) copy-start(f32[768]{0:T(1024)} %get-tuple-element.111) | copy-start | bytes 9220
  367.4 3.5 copy-start.1
  367.9 3.0 copy-start.76
  370.0 3.5 slice-start.5
  373.5 8.0 %copy-start.18 = (bf16[1024,768]{0,1:T(8,128)(2,1)}, bf16[1024,768]{0,1:T(8,128)(2,1)S(1)}, u32[]{:S(2)}) copy-start(bf16[1024,768]{0,1:T(8,128)(2,1)S(1)} %get-tuple-element.118) | copy-start | bytes 4718596
  415.4 2.9 copy-start.70
  415.5 2.9 copy-start.72
  415.5 4.0 copy-start.80
  434.3 3.5 copy-start.14
  434.4 3.5 copy-start.42
  434.4 3.7 copy-start.31
  436.0 3.1 copy-start.29
  436.0 4.2 copy-start.12
  436.1 4.2 copy-start.55
  440.3 6.4 copy-start.3
  440.3 6.4 copy-start.22
  446.7 8.8 %slice-start = ((s8[12582912]{0:T(1024)(128)(4,1)}), s8[4194304]{0:T(1024)(128)(4,1)S(1)}, s32[]{:S(2)}) async-start(s8[12582912]{0:T(1024)(128)(4,1)} %bitcast.239), calls=%async_computation.5 | async-start | bytes 8388608
  448.1 7.4 %slice-start.1 = ((s8[12582912]{0:T(1024)(128)(4,1)}), s8[4194304]{0:T(1024)(128)(4,1)S(1)}, s32[]{:S(2)}) async-start(s8[12582912]{0:T(1024)(128)(4,1)} %bitcast.239), calls=%async_computation.6 | async-start | bytes 8388608
  450.0 5.5 slice-start.2
  450.7 4.8 copy-start.15
  450.7 4.8 copy-start.39
  479.8 10.7 %copy-start.33 = (bf16[128,12,64]{0,2,1:T(8,128)(2,1)S(1)}, bf16[128,12,64]{0,2,1:T(8,128)(2,1)}, u32[]{:S(2)}) copy-start(bf16[128,12,64]{0,2,1:T(8,128)(2,1)} %fusion.66) | copy-start | bytes 589828
  493.0 7.7 %slice-start.3 = ((s8[6291456]{0:T(1024)(128)(4,1)}), s8[2097152]{0:T(1024)(128)(4,1)S(1)}, s32[]{:S(2)}) async-start(s8[6291456]{0:T(1024)(128)(4,1)} %bitcast.257), calls=%async_computation.8 | async-start | bytes 4194304
  493.6 6.0 copy-start.7
  493.6 5.0 copy-start.41
  493.6 7.1 %slice-start.4 = ((s8[6291456]{0:T(1024)(128)(4,1)}), s8[4194304]{0:T(1024)(128)(4,1)S(1)}, s32[]{:S(2)}) async-start(s8[6291456]{0:T(1024)(128)(4,1)} %bitcast.257), calls=%async_computation.9 | async-start | bytes 8388608
  503.4 6.9 %copy-start.4 = (f32[1024,768]{0,1:T(8,128)S(1)}, f32[1024,768]{0,1:T(8,128)}, u32[]{:S(2)}) copy-start(f32[1024,768]{0,1:T(8,128)} %get-tuple-element.139) | copy-start | bytes 9437188
  503.4 6.9 %copy-start.46 = (f32[1024]{0:T(1024)S(1)}, f32[1024]{0:T(1024)}, u32[]{:S(2)}) copy-start(f32[1024]{0:T(1024)} %copy-done.45) | copy-start | bytes 12292
  503.4 6.9 %copy-start.54 = (f32[1024]{0:T(1024)S(1)}, f32[1024]{0:T(1024)}, u32[]{:S(2)}) copy-start(f32[1024]{0:T(1024)} %copy-done.52) | copy-start | bytes 12292
  503.4 6.9 %copy-start.71 = (f32[1024]{0:T(1024)S(1)}, f32[1024]{0:T(1024)}, u32[]{:S(2)}) copy-start(f32[1024]{0:T(1024)} %copy-done.70) | copy-start | bytes 12292
  503.4 6.9 %copy-start.73 = (f32[1024]{0:T(1024)S(1)}, f32[1024]{0:T(1024)}, u32[]{:S(2)}) copy-start(f32[1024]{0:T(1024)} %copy-done.72) | copy-start | bytes 12292
  512.7 130.3 %copy-start.32 = (f32[8,6912]{1,0:T(8,128)S(1)}, f32[8,6912]{1,0:T(8,128)}, u32[]{:S(2)}) copy-start(f32[8,6912]{1,0:T(8,128)} %param.25) | copy-start | bytes 663556
  512.7 130.3 %copy-start.43 = (f32[8,6912]{1,0:T(8,128)S(1)}, f32[8,6912]{1,0:T(8,128)}, u32[]{:S(2)}) copy-start(f32[8,6912]{1,0:T(8,128)} %param.27) | copy-start | bytes 663556
  512.7 130.4 %copy-start.44 = (f32[8,6912]{1,0:T(8,128)S(1)}, f32[8,6912]{1,0:T(8,128)}, u32[]{:S(2)}) copy-start(f32[8,6912]{1,0:T(8,128)} %param.26) | copy-start | bytes 663556
  (32 other events, 60.1 us)
Sparse Core Ops, SparseCore 0:
  11.4 60.8 all-gather.7
  75.2 52.5 all-gather.9
  131.3 63.4 all-gather.11
  198.1 62.1 all-gather.13
  503.5 137.1 all-reduce.1
where the time goes:
time: 659 us; the launch traced here: 655 us
  blocking collectives  251 us (38%)
  matrix products  168 us (25%)
  waiting for transfers between devices  124 us (19%)
  local copies, waits for them, and re-layouts  54 us (8%)
  other arithmetic  41 us (6%)
  between operations  17.3 us (3%)
    psum x1, waiting for transfers between devices, on_device(): b_grad = lax.psum(local_gradient, ('dp', 'fsdp'))  124 us
    all_gather x1, blocking collectives, on_device(): lax.all_gather(ln_gains.astype(brain_float_type), ('dp', 'fsdp'), axis=1,...  66 us
    all_gather x1, blocking collectives, on_device(): lax.all_gather(ln_biases.astype(brain_float_type), ('dp', 'fsdp'), axis=1...  64 us
    all_gather x1, blocking collectives, on_device(): lax.all_gather(a_down.astype(brain_float_type), ('dp', 'fsdp'), axis=0, t...  63.5 us
    dot_general x11, matrix products, transposed_product(): lax.dot_general(left, right, (((1,), (1,)), ((), ())), preferred_element_...  63.5 us
    all_gather x1, blocking collectives, on_device(): lax.all_gather(a_in.astype(brain_float_type), ('dp', 'fsdp'), axis=0, til...  57.2 us
    dot_general x14, matrix products, product_result(): return jnp.dot(left, right, preferred_element_type=jnp.float32)  47 us
    unnamed x188, local copies, waits for them, and re-layouts  22.4 us
  transfers between devices with their start and end apart: 5, of which 1 were waited for; matrix products, arithmetic and copies ran while one was open for 16% of the time, Pallas kernels for 0%

commit v1 on v0

--- a/solution.py
+++ b/solution.py
@@ -1,3 +1,4 @@
+import functools
 import jax
 import jax.numpy as jnp
 from jax import lax
@@ -13,6 +14,13 @@
 beta_two = 0.98
 learn_rate = 0.02
 decay_rate = 0.01
+
+
+def _pack_domain(field, comm_axis):
+    return jnp.sum(lax.all_gather(field, comm_axis), axis=0)
+
+
+return_all_files_in = functools.partial(_pack_domain, comm_axis=("dp", "fsdp"))
 
 
 def bucket_plan(full):
@@ -376,7 +384,7 @@
         ],
         axis=1,
     )
-    b_grad = lax.psum(local_gradient, ("dp", "fsdp"))
+    b_grad = return_all_files_in(local_gradient)
     grad_norm = jnp.sqrt(jnp.sum(b_grad * b_grad))
     moment_new, second_new, adapter_new = adam_update(
         b_grad, grad_norm, moment_one, moment_two, adapter_b

time: 659 us -> 603 us (0.915)
  waiting for transfers between devices: 124 us -> 63.7 us
    psum x1 -> x0, waiting for transfers between devices: 124 us -> none  [on_device(): b_grad = lax.psum(local_gradient, ('dp', 'fsdp'))]
    all_gather x0 -> x1, waiting for transfers between devices: none -> 63.6 us  [_pack_domain(): return jnp.sum(lax.all_gather(field, comm_axis), axis=0)]
    unnamed x188 -> x189, local copies, waits for them, and re-layouts: 22.4 us -> 24 us
  transfers between devices with their start and end apart: 5 -> 5, of which waited for: 1 -> 1; matrix products, arithmetic and copies ran while one was open for 16% -> 18% of each run, Pallas kernels for 0% -> 0%
where the time goes in v1:
time: 603 us; the launch traced here: 597 us
  blocking collectives  251 us (42%)
  matrix products  167 us (28%)
  waiting for transfers between devices  63.7 us (11%)
  local copies, waits for them, and re-layouts  55.6 us (9%)
  other arithmetic  42.5 us (7%)
  between operations  17.1 us (3%)
    all_gather x1, blocking collectives, on_device(): lax.all_gather(ln_gains.astype(brain_float_type), ('dp', 'fsdp'), axis=1,...  66.2 us
    all_gather x1, blocking collectives, on_device(): lax.all_gather(ln_biases.astype(brain_float_type), ('dp', 'fsdp'), axis=1...  63.8 us
    all_gather x1, waiting for transfers between devices, _pack_domain(): return jnp.sum(lax.all_gather(field, comm_axis), axis=0)  63.6 us
    all_gather x1, blocking collectives, on_device(): lax.all_gather(a_down.astype(brain_float_type), ('dp', 'fsdp'), axis=0, t...  63.5 us
    dot_general x11, matrix products, transposed_product(): lax.dot_general(left, right, (((1,), (1,)), ((), ())), preferred_element_...  63.1 us
    all_gather x1, blocking collectives, on_device(): lax.all_gather(a_in.astype(brain_float_type), ('dp', 'fsdp'), axis=0, til...  57.2 us
    dot_general x14, matrix products, product_result(): return jnp.dot(left, right, preferred_element_type=jnp.float32)  46.7 us
    unnamed x189, local copies, waits for them, and re-layouts  24 us
  transfers between devices with their start and end apart: 5, of which 1 were waited for; matrix products, arithmetic and copies ran while one was open for 18% of the time, Pallas kernels for 0%

profile of v1, /device:TPU:8, one launch (start us, length us, event | category | flops | bytes accessed | tf_op | source)
XLA Modules:
  0.0 597.0 jit_solution(18318769336345957307)
XLA Ops:
  7.2 1.7 convert_element_type.392
  10.6 1.6 convert_element_type.423
  12.3 1.6 convert_element_type.426
  22.8 57.2 %all_gather.36 = bf16[768,40]{1,0:T(8,128)(2,1)S(1)} all-gather(bf16[24,40]{1,0:T(8,128)(2,1)S(1)} %convert_element_type.393), channel_id=1, replica_groups=mesh['dp'=8,'fsdp'=4] {'dp','fsdp'}, dimensions={0}, use_global_device_ids=true | all-gather | bytes 63360 | tf_op jit(solution)/shard_map/all_gather | solution.py:223
  82.1 2.3 fusion.131
  84.4 2.4 fusion.134
  86.8 2.2 fusion.137
  89.9 63.8 %all-gather.1 = bf16[32,24,2]{1,2,0:T(2,128)(2,1)S(1)} all-gather(bf16[1,24,2]{1,2,0:T(2,128)(2,1)S(1)} %convert_bitcast_fusion.1), channel_id=1, replica_groups=mesh['dp'=8,'fsdp'=4] {'dp','fsdp'}, dimensions={0}, use_global_device_ids=true | all-gather | bytes 3168 | tf_op jit(solution)/shard_map/all_gather | solution.py:226
  153.7 66.2 %all-gather = bf16[32,24,2]{1,2,0:T(2,128)(2,1)S(1)} all-gather(bf16[1,24,2]{1,2,0:T(2,128)(2,1)S(1)} %convert_bitcast_fusion.2), channel_id=1, replica_groups=mesh['dp'=8,'fsdp'=4] {'dp','fsdp'}, dimensions={0}, use_global_device_ids=true | all-gather | bytes 3168 | tf_op jit(solution)/shard_map/all_gather | solution.py:225
  221.6 63.5 %all-gather.2 = bf16[32,96,8]{1,2,0:T(8,128)(2,1)S(1)} all-gather(bf16[1,96,8]{1,2,0:T(8,128)(2,1)S(1)} %convert_bitcast_fusion), channel_id=1, replica_groups=mesh['dp'=8,'fsdp'=4] {'dp','fsdp'}, dimensions={0}, use_global_device_ids=true | all-gather | bytes 50688 | tf_op jit(solution)/shard_map/all_gather | solution.py:224
  288.2 8.8 %fusion.9 = bf16[1024,2304]{1,0:T(8,128)(2,1)} fusion(f32[1024,768]{1,0:T(8,128)} %fusion.131, f32[1024,768]{1,0:T(8,128)} %fusion.134, f32[1024,768]{1,0:T(8,128)} %fusion.137, bf16[1024,768]{1,0:T(8,128)(2,1)S(1)} %copy-done.18, bf16[768,2304]{1,0:T(8,128)(2,1)} %all-gather.9.cloned.1.call-done), kind=kOutput, calls=%fused_computation.20 | convolution fusion | flops 3635675136 | bytes 19267584 | tf_op jit(solution)/shard_map/dot_general | solution.py:46
  297.0 6.6 %copy.153 = bf16[1024,2304]{0,1:T(8,128)(2,1)} copy(bf16[1024,2304]{1,0:T(8,128)(2,1)} %fusion.9) | data formatting | bytes 9437184 | tf_op jit(solution)/shard_map/convert_element_type | solution.py:264
  312.3 1.9 fusion.168
  314.2 5.1 fusion.169
  319.8 2.0 fusion.48
  321.8 2.0 copy-done.65
  323.8 1.8 fusion.6
  325.6 4.1 fusion.26
  330.1 2.8 fusion.111
  338.5 7.5 %fusion.174 = f32[1024,3072]{1,0:T(8,128)S(1)} fusion(bf16[1024,768]{0,1:T(8,128)(2,1)} %copy-done.9, bf16[768,3072]{1,0:T(8,128)(2,1)} %all-gather.13.cloned.1.call-done), kind=kOutput, calls=%fused_computation.259 | convolution fusion | flops 4831838208 | bytes 18874368 | tf_op jit(solution)/shard_map/dot_general | solution.py:46
  346.0 6.9 %multiply_convert_fusion.1 = (bf16[1024,3072]{1,0:T(8,128)(2,1)S(1)}, f32[1024,3072]{1,0:T(8,128)}) fusion(f32[1024,3072]{1,0:T(8,128)S(1)} %fusion.174, bf16[1024,8]{0,1:T(8,128)(2,1)S(1)} %convolution_convert_fusion.6, bf16[8,6912]{1,0:T(8,128)(2,1)S(1)} %convert_element_type.395), kind=kOutput, calls=%fused_computation.10 | convolution fusion | flops 72351744 | bytes 31522816 | tf_op jit(solution)/shard_map/dot_general | solution.py:46
  352.9 2.7 copy-done.6
  355.6 1.7 convolution_convert_fusion.5
  357.3 8.8 %fusion.175 = f32[1024,768]{0,1:T(8,128)S(1)} fusion(bf16[1024,3072]{1,0:T(8,128)(2,1)} %copy-done.6, bf16[3072,768]{1,0:T(8,128)(2,1)} %all-gather.15.cloned.1.call-done), kind=kOutput, calls=%fused_computation.260 | convolution fusion | flops 4831838208 | bytes 14155776 | tf_op jit(solution)/shard_map/dot_general | solution.py:46
  367.7 2.1 copy-done.5
  370.7 2.6 fusion.120
  373.4 8.1 %fusion.176 = f32[1024,3072]{1,0:T(8,128)} fusion(bf16[1024,768]{0,1:T(8,128)(2,1)S(1)} %get-tuple-element.118, bf16[3072,768]{1,0:T(8,128)(2,1)S(1)} %bitcast.304), kind=kOutput, calls=%fused_computation.261 | convolution fusion | flops 4831838208 | bytes 18874368 | tf_op jit(solution)/shard_map/dot_general | solution.py:50
  381.4 13.7 %fusion.5 = bf16[1024,3072]{1,0:T(8,128)(2,1)} fusion(f32[1024,3072]{1,0:T(8,128)} %get-tuple-element.136, f32[1024,3072]{1,0:T(8,128)} %fusion.176, bf16[3072,8]{0,1:T(8,128)(2,1)S(1)} %copy-done.48, bf16[1024,768]{0,1:T(8,128)(2,1)} %copy-done.19, bf16[8,6912]{1,0:T(8,128)(2,1)S(1)} %convert_element_type.395), kind=kOutput, calls=%fused_computation.6 | convolution fusion | flops 97533952 | bytes 33091584 | tf_op jit(solution)/shard_map/dot_general | solution.py:50
  395.1 10.0 %fusion.177 = f32[1024,768]{0,1:T(8,128)} fusion(bf16[1024,3072]{1,0:T(8,128)(2,1)} %fusion.5, bf16[768,3072]{1,0:T(8,128)(2,1)} %all-gather.13.cloned.1.call-done), kind=kOutput, calls=%fused_computation.262 | convolution fusion | flops 4831838208 | bytes 14155776 | tf_op jit(solution)/shard_map/dot_general | solution.py:50
  405.1 10.2 %fusion.161 = (f32[1024]{0:T(1024)S(1)}, f32[1024]{0:T(1024)S(1)}, f32[1024,768]{0,1:T(8,128)}) fusion(f32[1024]{0:T(1024)S(1)} %copy-done.54, f32[1024,768]{0,1:T(8,128)S(1)} %get-tuple-element.134, f32[1024]{0:T(1024)S(1)} %broadcast_multiply_fusion.6, f32[768]{0:T(1024)S(1)} %copy-done.63, bf16[768,40]{1,0:T(8,128)(2,1)S(1)} %all_gather.36, ...), kind=kOutput, calls=%fused_computation.249 | convolution fusion | flops 76298240 | bytes 20738048 | tf_op jit(solution)/shard_map/dot_general | solution.py:50
  415.4 2.8 fusion.96
  419.4 3.0 fusion.178
  422.4 4.4 add_convert_fusion.1
  426.8 1.8 slice.306
  428.6 1.7 fusion.164
  430.3 2.1 slice.305
  432.4 1.9 reshape.820
  434.2 1.7 fusion.55
  436.0 1.7 multiply_reduce_fusion.6
  442.7 2.0 fusion.65
  444.7 1.8 fusion.66
  447.9 1.9 multiply_reduce_fusion.1
  450.6 2.6 fusion.56
  453.2 2.2 fusion.57
  455.4 3.3 fusion.39
  458.7 7.2 %multiply_reduce_fusion = (f32[12,512]{1,0:T(8,128)S(1)}, f32[12,512,512]{1,2,0:T(8,128)}) fusion(f32[12,512,512]{1,2,0:T(8,128)S(1)} %bitcast.264, f32[12,512]{1,0:T(8,128)S(1)} %copy-done.40, bf16[512,12,64]{0,2,1:T(8,128)(2,1)S(1)} %bitcast.291, bf16[1,1024,3,12,64]{1,4,3,2,0:T(8,128)(2,1)} %bitcast.278), kind=kOutput, calls=%fused_computation.8 | convolution fusion | flops 412084224 | bytes 26787840 | tf_op jit(solution)/shard_map/while/body/eval_jaxpr/gqhe,gkhe->ghqk/dot_general | solution.py:110
  465.8 6.8 %multiply_convert_fusion = bf16[12,512,512]{1,2,0:T(8,128)(2,1)S(1)} fusion(f32[12,512,512]{1,2,0:T(8,128)} %get-tuple-element.147, f32[12,512,512]{1,2,0:T(8,128)S(1)} %bitcast.264, f32[12,512]{1,0:T(8,128)S(1)} %get-tuple-element.146, f32[12,512]{1,0:T(8,128)S(1)} %copy-done.40), kind=kLoop, calls=%fused_computation.7 | loop fusion | flops 12582912 | bytes 31506432 | tf_op jit(solution)/shard_map/while/body/eval_jaxpr/convert_element_type | solution.py:114
  472.6 4.0 fusion.44
  476.7 3.2 fusion.43
  481.0 1.9 reshape.829
  482.9 1.9 copy.176
  484.8 1.9 reshape.821
  486.7 1.9 copy.183
  488.6 1.9 reshape.825
  490.6 1.7 maximum_bitcast_fusion.2
  500.6 2.7 copy.192
  503.4 1.9 fusion.29
  505.2 1.7 fusion.33
  507.0 1.7 fusion.37
  508.8 6.0 %fusion.179 = f32[1024,768]{0,1:T(8,128)S(1)} fusion(bf16[768,2304]{1,0:T(8,128)(2,1)} %all-gather.9.cloned.1.call-done, bf16[1024,2304]{0,1:T(8,128)(2,1)S(1)} %bitcast.289), kind=kOutput, calls=%fused_computation.264 | convolution fusion | flops 3623878656 | bytes 11403264 | tf_op jit(solution)/shard_map/dot_general | solution.py:50
  514.8 2.4 add_convert_fusion
  517.2 2.6 copy.193
  519.8 63.6 %all-gather.17.cloned.1.call-done = f32[32,8,6912]{2,1,0:T(8,128)} async-done(((f32[1,8,6912]{2,1,0:T(8,128)}), f32[32,8,6912]{2,1,0:T(8,128)}) %all-gather.17.cloned.1.call-update) | async-done | bytes 7077904 | tf_op jit(solution)/shard_map/all_gather | solution.py:20
  583.4 3.3 reduce_sum.186
  (286 shorter events, 54.6 us)
Async XLA Ops:
  7.2 72.8 %copy-start.18 = (bf16[1024,768]{1,0:T(8,128)(2,1)S(1)}, bf16[1024,768]{1,0:T(8,128)(2,1)}, u32[]{:S(2)}) copy-start(bf16[1024,768]{1,0:T(8,128)(2,1)} %param.14) | copy-start | bytes 4718596
  7.2 281.0 %all-gather.9.cloned.1.call-start = ((), (), s32[]{:S(2)}) async-start(), calls=%async_computation | async-start | bytes 3649536 | tf_op jit(solution)/shard_map/all_gather | solution.py:217
  8.9 321.2 %all-gather.11.cloned.1.call-start = ((), (), s32[]{:S(2)}) async-start(), calls=%async_computation.1 | async-start | bytes 1216512 | tf_op jit(solution)/shard_map/all_gather | solution.py:220
  10.5 328.0 %all-gather.13.cloned.1.call-start = ((), (), s32[]{:S(2)}) async-start(), calls=%async_computation.2 | async-start | bytes 4866048 | tf_op jit(solution)/shard_map/all_gather | solution.py:221
  12.2 345.1 %all-gather.15.cloned.1.call-start = ((), (), s32[]{:S(2)}) async-start(), calls=%async_computation.3 | async-start | bytes 4866048 | tf_op jit(solution)/shard_map/all_gather | solution.py:222
  14.0 569.4 %all-gather.17.cloned.1.call-start = ((), (), s32[]{:S(2)}) async-start(), calls=%async_computation.4 | async-start | bytes 7299072 | tf_op jit(solution)/shard_map/all_gather | solution.py:20
  22.8 399.6 %copy-start.39 = (bf16[8,6912]{1,0:T(8,128)(2,1)}, bf16[8,6912]{1,0:T(8,128)(2,1)S(1)}, u32[]{:S(2)}) copy-start(bf16[8,6912]{1,0:T(8,128)(2,1)S(1)} %convert_element_type.395) | copy-start | bytes 331780
  82.1 4.7 copy-start.41
  84.4 5.4 copy-start.82
  84.4 5.4 copy-start.83
  84.4 5.5 copy-start.78
  84.4 201.5 %copy-start.27 = (bf16[1024,768]{1,0:T(8,128)(2,1)S(1)}, bf16[1024,768]{1,0:T(8,128)(2,1)}, u32[]{:S(2)}) copy-start(bf16[1024,768]{1,0:T(8,128)(2,1)} %param.15) | copy-start | bytes 4718596
  220.8 115.6 %copy-start.62 = (f32[768]{0:T(1024)}, f32[768]{0:T(1024)S(1)}, u32[]{:S(2)}) copy-start(f32[768]{0:T(1024)S(1)} %get-tuple-element.109) | copy-start | bytes 9220
  305.0 5.0 copy-start.29
  305.2 4.8 copy-start.31
  305.4 4.6 copy-start.84
  305.8 4.8 copy-start.28
  314.2 5.6 copy-start.2
  319.3 6.2 %copy-start = (f32[12,512,512]{1,2,0:T(8,128)}, f32[12,512,512]{1,2,0:T(8,128)S(1)}, u32[]{:S(2)}) copy-start(f32[12,512,512]{1,2,0:T(8,128)S(1)} %get-tuple-element.132) | copy-start | bytes 37748740
  319.8 4.0 copy-start.65
  325.5 4.2 copy-start.57
  330.1 2.9 copy-start.21
  333.9 81.5 %copy-start.46 = (f32[1024]{0:T(1024)}, f32[1024]{0:T(1024)S(1)}, u32[]{:S(2)}) copy-start(f32[1024]{0:T(1024)S(1)} %broadcast_multiply_fusion.6) | copy-start | bytes 12292
  334.5 3.9 copy-start.53
  338.5 7.5 %copy-start.49 = (bf16[1024,8]{0,1:T(8,128)(2,1)}, bf16[1024,8]{0,1:T(8,128)(2,1)S(1)}, u32[]{:S(2)}) copy-start(bf16[1024,8]{0,1:T(8,128)(2,1)S(1)} %convolution_convert_fusion.6) | copy-start | bytes 49156
  346.0 9.6 %copy-start.48 = (bf16[3072,8]{0,1:T(8,128)(2,1)S(1)}, bf16[3072,8]{0,1:T(8,128)(2,1)}, u32[]{:S(2)}) copy-start(bf16[3072,8]{0,1:T(8,128)(2,1)} %reshape.837) | copy-start | bytes 147460
  357.3 8.9 %copy-start.51 = (bf16[1024,8]{0,1:T(8,128)(2,1)}, bf16[1024,8]{0,1:T(8,128)(2,1)S(1)}, u32[]{:S(2)}) copy-start(bf16[1024,8]{0,1:T(8,128)(2,1)S(1)} %convolution_convert_fusion.5) | copy-start | bytes 49156
  357.3 8.9 %copy-start.54 = (f32[1024]{0:T(1024)S(1)}, f32[1024]{0:T(1024)}, u32[]{:S(2)}) copy-start(f32[1024]{0:T(1024)} %copy-done.53) | copy-start | bytes 12292
  357.3 8.9 %copy-start.63 = (f32[768]{0:T(1024)S(1)}, f32[768]{0:T(1024)}, u32[]{:S(2)}) copy-start(f32[768]{0:T(1024)} %copy-done.62) | copy-start | bytes 9220
  357.3 8.9 %copy-start.70 = (f32[768]{0:T(1024)S(1)}, f32[768]{0:T(1024)}, u32[]{:S(2)}) copy-start(f32[768]{0:T(1024)} %get-tuple-element.111) | copy-start | bytes 9220
  367.3 3.5 copy-start.1
  367.7 3.0 copy-start.77
  369.8 3.5 slice-start.5
  373.3 8.1 %copy-start.19 = (bf16[1024,768]{0,1:T(8,128)(2,1)}, bf16[1024,768]{0,1:T(8,128)(2,1)S(1)}, u32[]{:S(2)}) copy-start(bf16[1024,768]{0,1:T(8,128)(2,1)S(1)} %get-tuple-element.118) | copy-start | bytes 4718596
  415.4 4.0 copy-start.81
  434.2 3.5 copy-start.15
  434.2 3.5 copy-start.43
  434.2 3.7 copy-start.32
  435.9 3.1 copy-start.30
  435.9 4.2 copy-start.13
  435.9 4.2 copy-start.56
  440.2 6.4 %copy-start.3 = (f32[12,256,256]{1,2,0:T(8,128)S(1)}, f32[12,256,256]{1,2,0:T(8,128)}, u32[]{:S(2)}) copy-start(f32[12,256,256]{1,2,0:T(8,128)} %copy-done.2) | copy-start | bytes 9437188
  440.2 6.4 %copy-start.22 = (bf16[256,768]{0,1:T(8,128)(2,1)S(1)}, bf16[256,768]{0,1:T(8,128)(2,1)}, u32[]{:S(2)}) copy-start(bf16[256,768]{0,1:T(8,128)(2,1)} %slice.306) | copy-start | bytes 1179652
  446.6 8.8 %slice-start = ((s8[12582912]{0:T(1024)(128)(4,1)}), s8[4194304]{0:T(1024)(128)(4,1)S(1)}, s32[]{:S(2)}) async-start(s8[12582912]{0:T(1024)(128)(4,1)} %bitcast.263), calls=%async_computation.5 | async-start | bytes 8388608
  447.9 7.4 %slice-start.1 = ((s8[12582912]{0:T(1024)(128)(4,1)}), s8[4194304]{0:T(1024)(128)(4,1)S(1)}, s32[]{:S(2)}) async-start(s8[12582912]{0:T(1024)(128)(4,1)} %bitcast.263), calls=%async_computation.6 | async-start | bytes 8388608
  449.9 5.4 slice-start.2
  450.5 4.8 copy-start.16
  450.6 4.8 copy-start.40
  479.8 10.7 %copy-start.34 = (bf16[128,12,64]{0,2,1:T(8,128)(2,1)S(1)}, bf16[128,12,64]{0,2,1:T(8,128)(2,1)}, u32[]{:S(2)}) copy-start(bf16[128,12,64]{0,2,1:T(8,128)(2,1)} %fusion.67) | copy-start | bytes 589828
  492.8 4.8 slice-start.3
  493.0 4.9 slice-start.4
  493.6 4.0 copy-start.7
  493.6 3.5 copy-start.11
  493.6 3.5 copy-start.60
  494.0 4.0 copy-start.50
  503.4 5.4 copy-start.8
  508.7 6.0 %copy-start.4 = (f32[1024,768]{0,1:T(8,128)S(1)}, f32[1024,768]{0,1:T(8,128)}, u32[]{:S(2)}) copy-start(f32[1024,768]{0,1:T(8,128)} %get-tuple-element.139) | copy-start | bytes 9437188
  508.7 6.0 %copy-start.47 = (f32[1024]{0:T(1024)S(1)}, f32[1024]{0:T(1024)}, u32[]{:S(2)}) copy-start(f32[1024]{0:T(1024)} %copy-done.46) | copy-start | bytes 12292
  508.7 6.0 %copy-start.55 = (f32[1024]{0:T(1024)S(1)}, f32[1024]{0:T(1024)}, u32[]{:S(2)}) copy-start(f32[1024]{0:T(1024)} %copy-done.53) | copy-start | bytes 12292
  508.7 6.0 %copy-start.72 = (f32[1024]{0:T(1024)S(1)}, f32[1024]{0:T(1024)}, u32[]{:S(2)}) copy-start(f32[1024]{0:T(1024)} %copy-done.71) | copy-start | bytes 12292
  508.7 6.0 %copy-start.74 = (f32[1024]{0:T(1024)S(1)}, f32[1024]{0:T(1024)}, u32[]{:S(2)}) copy-start(f32[1024]{0:T(1024)} %copy-done.73) | copy-start | bytes 12292
  519.8 68.4 %copy-start.33 = (f32[8,6912]{1,0:T(8,128)S(1)}, f32[8,6912]{1,0:T(8,128)}, u32[]{:S(2)}) copy-start(f32[8,6912]{1,0:T(8,128)} %param.25) | copy-start | bytes 663556
  519.8 68.4 %copy-start.44 = (f32[8,6912]{1,0:T(8,128)S(1)}, f32[8,6912]{1,0:T(8,128)}, u32[]{:S(2)}) copy-start(f32[8,6912]{1,0:T(8,128)} %param.27) | copy-start | bytes 663556
  519.8 68.4 %copy-start.45 = (f32[8,6912]{1,0:T(8,128)S(1)}, f32[8,6912]{1,0:T(8,128)}, u32[]{:S(2)}) copy-start(f32[8,6912]{1,0:T(8,128)} %param.26) | copy-start | bytes 663556
  (33 other events, 61.7 us)
Sparse Core Ops, SparseCore 0:
  11.4 60.8 all-gather.8
  75.3 52.5 all-gather.10
  131.3 63.4 all-gather.12
  198.1 62.0 all-gather.14
  500.7 82.6 all-gather.16
